TPU v7x, 32 devices: a whole 2x2x4 slice. The times are simulated.
32 devices in a mesh: fsdp: 4 (over y, x), ctx: 8 (over z, core).
Axes of the slice: x: 2, y: 2, z: 4, core: 2. Of those that a mesh axis runs over, the one named last changes fastest.
Arguments:
- layer_input: bfloat16 [4, 1024, 1600], P('fsdp', 'ctx'), may hold values from -6 to 6
- pair_blocks: int32 [8, 2], replicated, may hold values from 0 to 15, as said below
- ln1_gain: bfloat16 [1600], P('fsdp'), may hold values from 0.25 to 1.75
- ln1_bias: bfloat16 [1600], P('fsdp'), may hold values from -3 to 3
- w_qkv: bfloat16 [1600, 4800], P('fsdp'), may hold values from -0.15625 to 0.15625
- bias_q: bfloat16 [1600], P('fsdp'), may hold values from -5 to 5
- bias_v: bfloat16 [1600], P('fsdp'), may hold values from -3 to 3
- w_proj: bfloat16 [1600, 1600], P('fsdp'), may hold values from -0.625 to 0.625
- bias_proj: bfloat16 [1600], P('fsdp'), may hold values from -3 to 3
- ln2_gain: bfloat16 [1600], P('fsdp'), may hold values from 0.25 to 1.75
- ln2_bias: bfloat16 [1600], P('fsdp'), may hold values from -3 to 3
- w_fc: bfloat16 [1600, 6400], P('fsdp'), may hold values from -0.15625 to 0.15625
- bias_fc: bfloat16 [6400], P('fsdp'), may hold values from -3 to 3
- w_out: bfloat16 [6400, 1600], P('fsdp'), may hold values from -0.078125 to 0.078125
- bias_out: bfloat16 [1600], P('fsdp'), may hold values from -3 to 3
- cotangent: bfloat16 [4, 1024, 1600], P('fsdp', 'ctx'), may hold values from -6 to 6
Outputs:
- output: bfloat16 [4, 1024, 1600], P('fsdp', 'ctx')
- grad_input: bfloat16 [4, 1024, 1600], P('fsdp', 'ctx')
- grad_ln1_gain: float32 [1600], P('fsdp')
- grad_ln1_bias: float32 [1600], P('fsdp')
- grad_w_qkv: float32 [1600, 4800], P('fsdp')
- grad_bias_q: float32 [1600], P('fsdp')
- grad_bias_v: float32 [1600], P('fsdp')
- grad_w_proj: float32 [1600, 1600], P('fsdp')
- grad_bias_proj: float32 [1600], P('fsdp')
- grad_ln2_gain: float32 [1600], P('fsdp')
- grad_ln2_bias: float32 [1600], P('fsdp')
- grad_w_fc: float32 [1600, 6400], P('fsdp')
- grad_bias_fc: float32 [6400], P('fsdp')
- grad_w_out: float32 [6400, 1600], P('fsdp')
- grad_bias_out: float32 [1600], P('fsdp')
Inputs may be any that keep to these rules, and one draw needn't show every extreme that they name: `pair_blocks`: row r is b and 15 - b for some b < 8; the first entries of the rows are a permutation of 0 to 7.
All inputs are finite; a program needn't handle non-finite values.
Results may differ from a plain program's by a relative error of at most 0.017.
Values may be sent and summed in bfloat16 or wider, within the bound.
A program may use at most 384 MiB of HBM per device.

v0:
```python
from functools import partial

import jax
import jax.numpy as jnp
from jax import lax
from jax.sharding import PartitionSpec as P

HEADS = 25
HEAD = 64


EPSILON = 1e-05
MASKED = -1e30


def matmul(left, right):
    return jnp.dot(left, right, preferred_element_type=jnp.float32)


def matmul_t(left, right):
    return lax.dot_general(
        left, right, (((1,), (1,)), ((), ())), preferred_element_type=jnp.float32
    )


def layer_norm(inputs, gain, shift):
    centred = inputs - jnp.mean(inputs, axis=-1, keepdims=True)
    inverse = lax.rsqrt(jnp.mean(centred * centred, axis=-1, keepdims=True) + EPSILON)
    normed = centred * inverse
    return (normed * gain + shift, normed, inverse)


def norm_back(grad_out, normed, inverse, gain):
    grad_norm = grad_out * gain
    mean_grad = jnp.mean(grad_norm, axis=-1, keepdims=True)
    mean_dot = jnp.mean(grad_norm * normed, axis=-1, keepdims=True)
    return inverse * (grad_norm - mean_grad - normed * mean_dot)


def gather_attention(ln1_gain, ln1_bias, w_qkv, bias_q, bias_v, w_proj, bias_proj):
    return (
        lax.all_gather(ln1_gain, "fsdp", axis=0, tiled=True),
        lax.all_gather(ln1_bias, "fsdp", axis=0, tiled=True),
        lax.all_gather(w_qkv, "fsdp", axis=0, tiled=True),
        lax.all_gather(bias_q, "fsdp", axis=0, tiled=True),
        lax.all_gather(bias_v, "fsdp", axis=0, tiled=True),
        lax.all_gather(w_proj, "fsdp", axis=0, tiled=True),
        lax.all_gather(bias_proj, "fsdp", axis=0, tiled=True),
    )


def gather_mlp(ln2_gain, ln2_bias, w_fc, bias_fc, w_out, bias_out):
    return (
        lax.all_gather(ln2_gain, "fsdp", axis=0, tiled=True),
        lax.all_gather(ln2_bias, "fsdp", axis=0, tiled=True),
        lax.all_gather(w_fc, "fsdp", axis=0, tiled=True),
        lax.all_gather(bias_fc, "fsdp", axis=0, tiled=True),
        lax.all_gather(w_out, "fsdp", axis=0, tiled=True),
        lax.all_gather(bias_out, "fsdp", axis=0, tiled=True),
    )


def gather_keys(key_rows, value_rows):
    return (
        lax.all_gather(key_rows, "ctx", axis=0, tiled=True),
        lax.all_gather(value_rows, "ctx", axis=0, tiled=True),
    )


def owned_rows(left, right):
    return lax.psum_scatter(
        lax.dot_general(left, right, (((0,), (0,)), ((), ())), preferred_element_type=jnp.float32),
        "fsdp",
        scatter_dimension=0,
        tiled=True,
    )


def tiles_of(all_keys, all_values, key_positions, tile_len):
    tile_count = all_keys.shape[0] // tile_len
    return (
        all_keys.reshape(tile_count, tile_len, HEADS, HEAD),
        all_values.reshape(tile_count, tile_len, HEADS, HEAD),
        key_positions.reshape(tile_count, tile_len),
    )


def attend(query_heads, key_tiles, query_positions):
    row_count = query_heads.shape[0]

    def step(carry, tile):
        top, total, accum = carry
        key_tile, value_tile, position_tile = tile
        score = jnp.einsum(
            "qhe,khe->hqk", query_heads, key_tile, preferred_element_type=jnp.float32
        )
        allowed = query_positions[None, :, None] >= position_tile[None, None, :]
        score = jnp.where(allowed, score, MASKED)
        new_top = jnp.maximum(top, jnp.max(score, axis=-1))
        probs = jnp.exp(score - new_top[..., None])
        factor = jnp.exp(top - new_top)
        total = total * factor + jnp.sum(probs, axis=-1)
        accum = accum * factor[..., None] + jnp.einsum(
            "hqk,khe->hqe",
            probs.astype(jnp.bfloat16),
            value_tile,
            preferred_element_type=jnp.float32,
        )
        return ((new_top, total, accum), None)

    start_carry = (
        jnp.full((HEADS, row_count), MASKED, jnp.float32),
        jnp.zeros((HEADS, row_count), jnp.float32),
        jnp.zeros((HEADS, row_count, HEAD), jnp.float32),
    )
    (top, total, accum), unused = lax.scan(step, start_carry, key_tiles)
    context = accum / total[..., None]
    return (jnp.transpose(context, (1, 0, 2)), top + jnp.log(total))


def attend_back(query_heads, key_tiles, query_positions, log_total, grad_heads, delta):
    row_count = query_heads.shape[0]

    def step(grad_query, tile):
        key_tile, value_tile, position_tile = tile
        score = jnp.einsum(
            "qhe,khe->hqk", query_heads, key_tile, preferred_element_type=jnp.float32
        )
        allowed = query_positions[None, :, None] >= position_tile[None, None, :]
        score = jnp.where(allowed, score, MASKED)
        probs = jnp.exp(score - log_total[..., None])
        grad_probs = jnp.einsum(
            "qhe,khe->hqk", grad_heads, value_tile, preferred_element_type=jnp.float32
        )
        grad_score = (probs * (grad_probs - delta[..., None])).astype(jnp.bfloat16)
        grad_query = grad_query + jnp.einsum(
            "hqk,khe->qhe", grad_score, key_tile, preferred_element_type=jnp.float32
        )
        grad_key = jnp.einsum(
            "hqk,qhe->khe", grad_score, query_heads, preferred_element_type=jnp.float32
        )
        grad_value = jnp.einsum(
            "hqk,qhe->khe",
            probs.astype(jnp.bfloat16),
            grad_heads,
            preferred_element_type=jnp.float32,
        )
        return (grad_query, (grad_key, grad_value))

    start_query = jnp.zeros((row_count, HEADS, HEAD), jnp.float32)
    grad_query, (key_terms, value_terms) = lax.scan(step, start_query, key_tiles)
    return (grad_query, key_terms, value_terms)


def shards(
    layer_input,
    pair_blocks,
    ln1_gain,
    ln1_bias,
    w_qkv,
    bias_q,
    bias_v,
    w_proj,
    bias_proj,
    ln2_gain,
    ln2_bias,
    w_fc,
    bias_fc,
    w_out,
    bias_out,
    cotangent,
):
    row_count = layer_input.shape[1]
    block_len = row_count // 2
    model_width = layer_input.shape[2]
    score_scale = HEAD ** (-0.5)
    ctx_index = lax.axis_index("ctx")
    own_blocks = lax.dynamic_index_in_dim(pair_blocks, ctx_index, 0, keepdims=False)
    offsets = jnp.arange(block_len, dtype=jnp.int32)
    query_positions = (own_blocks[:, None] * block_len + offsets[None, :]).reshape(row_count)
    key_positions = (pair_blocks[:, :, None] * block_len + offsets[None, None, :]).reshape(-1)
    tile_len = min(512, key_positions.shape[0])
    attention_params = gather_attention(
        ln1_gain, ln1_bias, w_qkv, bias_q, bias_v, w_proj, bias_proj
    )
    gain_one, shift_one, full_qkv, full_bias_q, full_bias_v, full_proj, full_bias_proj = (
        attention_params
    )
    stream = layer_input[0].astype(jnp.float32)
    normed_out, normed_one, inverse_one = layer_norm(
        stream, gain_one.astype(jnp.float32), shift_one.astype(jnp.float32)
    )
    normed_low = normed_out.astype(jnp.bfloat16)
    projected = matmul(normed_low, full_qkv)
    query_rows = (
        (projected[:, :model_width] + full_bias_q.astype(jnp.float32)) * score_scale
    ).astype(jnp.bfloat16)
    key_rows = projected[:, model_width : 2 * model_width].astype(jnp.bfloat16)
    value_rows = (projected[:, 2 * model_width :] + full_bias_v.astype(jnp.float32)).astype(
        jnp.bfloat16
    )
    all_keys, all_values = gather_keys(key_rows, value_rows)
    key_tiles = tiles_of(all_keys, all_values, key_positions, tile_len)
    query_heads = query_rows.reshape(row_count, HEADS, HEAD)
    context_heads, log_total = attend(query_heads, key_tiles, query_positions)
    context_full = context_heads.reshape(row_count, model_width)
    context_low = context_full.astype(jnp.bfloat16)
    mixed = stream + matmul(context_low, full_proj) + full_bias_proj.astype(jnp.float32)
    mlp_params = gather_mlp(ln2_gain, ln2_bias, w_fc, bias_fc, w_out, bias_out)
    gain_two, shift_two, full_fc, full_bias_fc, full_out, full_bias_out = mlp_params
    second_out, normed_two, inverse_two = layer_norm(
        mixed, gain_two.astype(jnp.float32), shift_two.astype(jnp.float32)
    )
    second_low = second_out.astype(jnp.bfloat16)
    hidden = matmul(second_low, full_fc) + full_bias_fc.astype(jnp.float32)
    activated = jax.nn.gelu(hidden, approximate=True).astype(jnp.bfloat16)
    result = (mixed + matmul(activated, full_out) + full_bias_out.astype(jnp.float32)).astype(
        jnp.bfloat16
    )
    again_mlp = gather_mlp(ln2_gain, ln2_bias, w_fc, bias_fc, w_out, bias_out)
    back_fc, back_out, back_gain_two = (again_mlp[2], again_mlp[4], again_mlp[0])
    grad_branch = cotangent[0]
    grad_out = grad_branch.astype(jnp.float32)
    grad_bias_out = jnp.sum(grad_out, axis=0)
    grad_act = matmul_t(grad_branch, back_out)
    unused_value, gelu_pull = jax.vjp(partial(jax.nn.gelu, approximate=True), hidden)
    grad_hidden = gelu_pull(grad_act)[0].astype(jnp.bfloat16)
    grad_bias_fc = jnp.sum(grad_hidden.astype(jnp.float32), axis=0)
    grad_second = matmul_t(grad_hidden, back_fc)
    grad_gain_two = jnp.sum(grad_second * normed_two, axis=0)
    grad_shift_two = jnp.sum(grad_second, axis=0)
    grad_mixed = grad_out + norm_back(
        grad_second, normed_two, inverse_two, back_gain_two.astype(jnp.float32)
    )
    grad_w_out = owned_rows(activated, grad_branch)
    grad_w_fc = owned_rows(second_low, grad_hidden)
    again_attention = gather_attention(ln1_gain, ln1_bias, w_qkv, bias_q, bias_v, w_proj, bias_proj)
    back_qkv, back_proj, back_gain_one = (
        again_attention[2],
        again_attention[5],
        again_attention[0],
    )
    again_keys, again_values = gather_keys(key_rows, value_rows)
    back_tiles = tiles_of(again_keys, again_values, key_positions, tile_len)
    grad_attended = grad_mixed.astype(jnp.bfloat16)
    grad_bias_proj = jnp.sum(grad_attended.astype(jnp.float32), axis=0)
    grad_context = matmul_t(grad_attended, back_proj).astype(jnp.bfloat16)
    grad_heads = grad_context.reshape(row_count, HEADS, HEAD)
    delta = jnp.transpose(jnp.sum(grad_heads.astype(jnp.float32) * context_heads, axis=-1))
    grad_query, key_terms, value_terms = attend_back(
        query_heads, back_tiles, query_positions, log_total, grad_heads, delta
    )
    grad_keys, grad_values = (
        lax.psum_scatter(
            key_terms.reshape(-1, model_width), "ctx", scatter_dimension=0, tiled=True
        ),
        lax.psum_scatter(
            value_terms.reshape(-1, model_width), "ctx", scatter_dimension=0, tiled=True
        ),
    )
    grad_w_proj = owned_rows(context_low, grad_attended)
    grad_query_low = grad_query.reshape(row_count, model_width).astype(jnp.bfloat16)
    grad_keys_low = grad_keys.astype(jnp.bfloat16)
    grad_values_low = grad_values.astype(jnp.bfloat16)
    grad_qkv = jnp.concatenate(
        [grad_query_low * jnp.bfloat16(score_scale), grad_keys_low, grad_values_low], axis=1
    )
    grad_bias_q = jnp.sum(grad_query_low.astype(jnp.float32), axis=0) * score_scale
    grad_bias_v = jnp.sum(grad_values_low.astype(jnp.float32), axis=0)
    grad_first = matmul_t(grad_qkv, back_qkv)
    grad_gain_one = jnp.sum(grad_first * normed_one, axis=0)
    grad_shift_one = jnp.sum(grad_first, axis=0)
    grad_stream = grad_mixed + norm_back(
        grad_first, normed_one, inverse_one, back_gain_one.astype(jnp.float32)
    )
    grad_w_qkv = owned_rows(normed_low, grad_qkv)
    small_grads = (
        lax.psum_scatter(grad_gain_one, "fsdp", scatter_dimension=0, tiled=True),
        lax.psum_scatter(grad_shift_one, "fsdp", scatter_dimension=0, tiled=True),
        lax.psum_scatter(grad_bias_q, "fsdp", scatter_dimension=0, tiled=True),
        lax.psum_scatter(grad_bias_v, "fsdp", scatter_dimension=0, tiled=True),
        lax.psum_scatter(grad_bias_proj, "fsdp", scatter_dimension=0, tiled=True),
        lax.psum_scatter(grad_gain_two, "fsdp", scatter_dimension=0, tiled=True),
        lax.psum_scatter(grad_shift_two, "fsdp", scatter_dimension=0, tiled=True),
        lax.psum_scatter(grad_bias_fc, "fsdp", scatter_dimension=0, tiled=True),
        lax.psum_scatter(grad_bias_out, "fsdp", scatter_dimension=0, tiled=True),
    )
    summed = lax.psum(
        (
            small_grads[0],
            small_grads[1],
            grad_w_qkv,
            small_grads[2],
            small_grads[3],
            grad_w_proj,
            small_grads[4],
            small_grads[5],
            small_grads[6],
            grad_w_fc,
            small_grads[7],
            grad_w_out,
            small_grads[8],
        ),
        "ctx",
    )
    return (
        result[None],
        grad_stream.astype(jnp.bfloat16)[None],
        summed[0],
        summed[1],
        summed[2],
        summed[3],
        summed[4],
        summed[5],
        summed[6],
        summed[7],
        summed[8],
        summed[9],
        summed[10],
        summed[11],
        summed[12],
    )


def solution(mesh):
    in_specs = (
        P("fsdp", "ctx", None),
        P(),
        P("fsdp"),
        P("fsdp"),
        P("fsdp", None),
        P("fsdp"),
        P("fsdp"),
        P("fsdp", None),
        P("fsdp"),
        P("fsdp"),
        P("fsdp"),
        P("fsdp", None),
        P("fsdp"),
        P("fsdp", None),
        P("fsdp"),
        P("fsdp", "ctx", None),
    )
    out_specs = (
        P("fsdp", "ctx", None),
        P("fsdp", "ctx", None),
        P("fsdp"),
        P("fsdp"),
        P("fsdp", None),
        P("fsdp"),
        P("fsdp"),
        P("fsdp", None),
        P("fsdp"),
        P("fsdp"),
        P("fsdp"),
        P("fsdp", None),
        P("fsdp"),
        P("fsdp", None),
        P("fsdp"),
    )
    return jax.shard_map(shards, mesh=mesh, in_specs=in_specs, out_specs=out_specs, check_vma=False)
```

profile of v0, /device:TPU:0, one launch (start us, length us, event | category | flops | bytes accessed | tf_op | source)
XLA Modules:
  0.0 3012.2 jit_solution(9673003929916029855)
XLA Ops:
  12.3 19.3 all-reduce.24
  32.2 127.9 %all-gather.7.cloned.1.call-done = bf16[1600,4800]{1,0:T(8,128)(2,1)} async-done(((bf16[400,4800]{1,0:T(8,128)(2,1)}), bf16[1600,4800]{1,0:T(8,128)(2,1)}) %all-gather.7.cloned.1.call-update) | async-done | bytes 15360016 | tf_op jit(solution)/shard_map/all_gather | solution.py:44
  160.1 10.6 fusion.102
  178.4 35.0 %all-gather.9.cloned.1.call-done = bf16[1024,1600]{0,1:T(8,128)(2,1)} async-done(((bf16[128,1600]{0,1:T(8,128)(2,1)}), bf16[1024,1600]{0,1:T(8,128)(2,1)}) %all-gather.9.cloned.1.call-update) | async-done | bytes 3276816 | tf_op jit(solution)/shard_map/all_gather | solution.py:65
  213.4 8.5 reshape.205
  226.2 27.8 all-gather.11.cloned.1.call-done
  254.0 8.5 reshape.207
  262.6 4.8 copy.57
  267.3 28.3 while.30
  267.6 5.5 fusion.150
  281.6 5.8 fusion.150
  295.8 20.2 all-gather.13.cloned.1.call-done
  316.0 4.8 fusion.106
  321.0 185.7 %all-gather.15.cloned.1.call-done = bf16[1600,6400]{1,0:T(8,128)(2,1)} async-done(((bf16[400,6400]{1,0:T(8,128)(2,1)}), bf16[1600,6400]{1,0:T(8,128)(2,1)}) %all-gather.15.cloned.1.call-update) | async-done | bytes 20480016 | tf_op jit(solution)/shard_map/all_gather | solution.py:56
  506.7 12.3 convolution_add_fusion
  519.0 185.2 %all-gather.17.cloned.1.call-done = bf16[6400,1600]{1,0:T(8,128)(2,1)} async-done(((bf16[1600,1600]{1,0:T(8,128)(2,1)}), bf16[6400,1600]{1,0:T(8,128)(2,1)}) %all-gather.17.cloned.1.call-update) | async-done | bytes 20480016 | tf_op jit(solution)/shard_map/all_gather | solution.py:58
  704.2 12.0 convert_reduce_fusion
  716.2 12.7 multiply_reduce_fusion
  735.3 292.4 %while.31 = (s32[]{:T(128)}, f32[128,25,64]{0,2,1:T(8,128)}, f32[2,512,25,64]{1,0,3,2:T(2,128)}, f32[2,512,25,64]{1,0,3,2:T(2,128)}, bf16[2,512,25,64]{1,3,2,0:T...) while((s32[]{:T(128)}, f32[128,25,64]{0,2,1:T(8,128)}, ...), condition=%wide.region_12.13_spmd.clone, body=%wide.region_11.12_spmd.clone.sunk | while | flops 1062158464 | bytes 70694584 | solution.py:151
  735.8 5.4 fusion.164
  741.5 5.7 fusion.165
  756.1 58.8 %dynamic_update_slice.11 = f32[2,512,25,64]{1,0,3,2:T(2,128)} dynamic-update-slice(f32[2,512,25,64]{1,0,3,2:T(2,128)} %get-tuple-element.559, f32[1,512,25,64]{1,0,3,2:T(1,128)S(1)} %copy.92, s32[]{:T(128)S(6)} %copy.121, s32[]{:T(128)} %constant.39.clone.1..sunk.1, s32[]{:T(128)} %constant.39.clone.1..sunk.1, s32[]{:T(128)} %constant.39.clone.1..sunk.1) | dynamic-update-slice | bytes 6553604 | tf_op jit(solution)/shard_map/while/body/jit(dynamic_update_index_in_dim)/dynamic_update_slice | solution.py:151
  814.9 4.5 fusion.167
  822.8 58.8 %dynamic_update_slice.12 = f32[2,512,25,64]{1,0,3,2:T(2,128)} dynamic-update-slice(f32[2,512,25,64]{1,0,3,2:T(2,128)} %get-tuple-element.560, f32[1,512,25,64]{1,0,3,2:T(1,128)S(1)} %copy.93, s32[]{:T(128)S(6)} %copy.121, s32[]{:T(128)} %constant.39.clone.1..sunk.1, s32[]{:T(128)} %constant.39.clone.1..sunk.1, s32[]{:T(128)} %constant.39.clone.1..sunk.1) | dynamic-update-slice | bytes 6553604 | tf_op jit(solution)/shard_map/while/body/jit(dynamic_update_index_in_dim)/dynamic_update_slice | solution.py:151
  881.6 5.4 fusion.164
  887.3 5.7 fusion.165
  902.1 58.8 %dynamic_update_slice.11 = f32[2,512,25,64]{1,0,3,2:T(2,128)} dynamic-update-slice(f32[2,512,25,64]{1,0,3,2:T(2,128)} %get-tuple-element.559, f32[1,512,25,64]{1,0,3,2:T(1,128)S(1)} %copy.92, s32[]{:T(128)S(6)} %copy.121, s32[]{:T(128)} %constant.39.clone.1..sunk.1, s32[]{:T(128)} %constant.39.clone.1..sunk.1, s32[]{:T(128)} %constant.39.clone.1..sunk.1) | dynamic-update-slice | bytes 6553604 | tf_op jit(solution)/shard_map/while/body/jit(dynamic_update_index_in_dim)/dynamic_update_slice | solution.py:151
  960.9 4.5 fusion.167
  968.8 58.8 %dynamic_update_slice.12 = f32[2,512,25,64]{1,0,3,2:T(2,128)} dynamic-update-slice(f32[2,512,25,64]{1,0,3,2:T(2,128)} %get-tuple-element.560, f32[1,512,25,64]{1,0,3,2:T(1,128)S(1)} %copy.93, s32[]{:T(128)S(6)} %copy.121, s32[]{:T(128)} %constant.39.clone.1..sunk.1, s32[]{:T(128)} %constant.39.clone.1..sunk.1, s32[]{:T(128)} %constant.39.clone.1..sunk.1) | dynamic-update-slice | bytes 6553604 | tf_op jit(solution)/shard_map/while/body/jit(dynamic_update_index_in_dim)/dynamic_update_slice | solution.py:151
  1027.8 7.2 copy.88
  1035.0 7.3 copy.89
  1043.5 5.7 fusion.98
  1050.5 56.9 %reduce-scatter.13.cloned.1.call-done = f32[128,1600]{0,1:T(8,128)} async-done(((f32[1024,1600]{0,1:T(8,128)}), f32[128,1600]{0,1:T(8,128)}) %reduce-scatter.13.cloned.1.call-update) | async-done | bytes 819216 | tf_op jit(solution)/shard_map/reduce_scatter | solution.py:254
  1108.5 72.4 %reduce-scatter.15.cloned.1.call-done = f32[128,1600]{0,1:T(8,128)} async-done(((f32[1024,1600]{0,1:T(8,128)}), f32[128,1600]{0,1:T(8,128)}) %reduce-scatter.15.cloned.1.call-update) | async-done | bytes 819216 | tf_op jit(solution)/shard_map/reduce_scatter | solution.py:257
  1183.8 13.3 fusion.87
  1198.2 18.9 fusion.104
  1218.1 19.6 fusion.90
  1238.7 10.0 fusion.81
  1248.8 40.6 %reduce-scatter.21.cloned.1.call-done = f32[400,1600]{1,0:T(8,128)} async-done(((f32[1600,1600]{1,0:T(8,128)}), f32[400,1600]{1,0:T(8,128)}) %reduce-scatter.21.cloned.1.call-update) | async-done | bytes 2560016
  1289.4 275.2 %reduce-scatter.19.cloned.1.call-done = f32[400,4800]{1,0:T(8,128)} async-done(((f32[1600,4800]{1,0:T(8,128)}), f32[400,4800]{1,0:T(8,128)}) %reduce-scatter.19.cloned.1.call-update) | async-done | bytes 7680016
  1564.6 391.2 %reduce-scatter.23.cloned.1.call-done = f32[400,6400]{1,0:T(8,128)} async-done(((f32[1600,6400]{1,0:T(8,128)}), f32[400,6400]{1,0:T(8,128)}) %reduce-scatter.23.cloned.1.call-update) | async-done | bytes 10240016
  1955.7 366.0 %reduce-scatter.17.cloned.1.call-done = f32[1600,1600]{1,0:T(8,128)} async-done(((f32[6400,1600]{1,0:T(8,128)}), f32[1600,1600]{1,0:T(8,128)}) %reduce-scatter.17.cloned.1.call-update) | async-done | bytes 10240016 | tf_op jit(solution)/shard_map/reduce_scatter | solution.py:71
  2323.7 14.7 fusion.66
  2339.5 32.3 %all-reduce.30.cloned.1.call-done = (f32[1600]{0:T(1024)}, f32[1600]{0:T(1024)}, f32[1600]{0:T(1024)}, f32[1600]{0:T(1024)}, f32[1600]{0:T(1024)}, /*index=5*/f3...) async-done(((f32[1600]{0:T(1024)}, f32[1600]{0:T(1024)}, f32[1600]{0:T(1024)}, f32[1600]{0:T(1024)}, f32[1600]{0:T(1024)}, /*index=5*/f32[1600]{0:T(1024)}, ...) | async-done | bytes 76816
  2378.8 30.5 %all-reduce.21 = (f32[400]{0:T(512)}, f32[400]{0:T(512)}, f32[400]{0:T(512)}, f32[400]{0:T(512)}, f32[400]{0:T(512)}, /*index=5*/f32[400]{0:T(512)}, f32[400]{0:T(512)}, f32[1600]{0:T(1024)}, f32[400]{0:T(512)}) all-reduce(f32[400]{0:T(512)S(1)} %dynamic-slice.10, ...), channel_id=1, replica_groups=mesh['fsdp'=4,'ctx'=8] {'ctx'}, use_global_device_ids=true, to_apply=%region_19.20 | all-reduce | flops 4800 | bytes 38400 | tf_op jit(solution)/shard_map/psum | solution.py:288
  2409.2 574.1 %all-reduce.28.cloned.1.call-done = (f32[400,4800]{1,0:T(8,128)}, f32[400,1600]{1,0:T(8,128)}, f32[400,6400]{1,0:T(8,128)}, f32[1600,1600]{1,0:T(8,128)}) async-done(((f32[400,4800]{1,0:T(8,128)}, f32[400,1600]{1,0:T(8,128)}, f32[400,6400]{1,0:T(8,128)}, f32[1600,1600]{1,0:T(8,128)}), (f32[400,4800]{1,0:T(8,128)}, f32[400,1600]{1,0:T(8,128)}, f32[400,6400]{1,0:T(8,128)}, ...) | async-done | bytes 30720016 | tf_op jit(solution)/shard_map/psum | solution.py:288
  2983.4 7.1 copy.142
  2991.9 9.3 copy.144
  (230 shorter events, 88.8 us)
Async XLA Ops:
  7.2 2.8 copy-start.34
  7.2 3.1 copy-start.35
  7.2 3.3 copy-start.36
  7.2 3.6 copy-start.37
  7.2 3.8 copy-start.38
  7.2 4.0 copy-start.39
  7.3 4.3 copy-start.40
  7.3 4.5 copy-start.41
  7.3 4.8 copy-start.31
  7.3 24.4 copy-start.5
  7.3 152.8 %all-gather.7.cloned.1.call-start = ((), (), s32[]{:S(2)}) async-start(), calls=%async_computation.6 | async-start | bytes 19456000 | tf_op jit(solution)/shard_map/all_gather | solution.py:44
  8.0 205.3 %all-gather.9.cloned.1.call-start = ((), (), s32[]{:S(2)}) async-start(), calls=%async_computation.7 | async-start | bytes 3686400 | tf_op jit(solution)/shard_map/all_gather | solution.py:65
  31.7 139.0 %copy-start.22 = (f32[1600]{0:T(1024)}, f32[1600]{0:T(1024)S(1)}, u32[]{:S(2)}) copy-start(f32[1600]{0:T(1024)S(1)} %convert_element_type.114) | copy-start | bytes 19204
  31.7 139.0 %copy-start.20 = (f32[1600]{0:T(1024)}, f32[1600]{0:T(1024)S(1)}, u32[]{:S(2)}) copy-start(f32[1600]{0:T(1024)S(1)} %convert_element_type.113) | copy-start | bytes 19204
  31.9 138.8 %copy-start.26 = (f32[128]{0:T(128)}, f32[128]{0:T(128)S(1)}, u32[]{:S(2)}) copy-start(f32[128]{0:T(128)S(1)} %broadcast_multiply_fusion.8) | copy-start | bytes 1540
  32.2 138.5 %copy-start.28 = (f32[128]{0:T(128)}, f32[128]{0:T(128)S(1)}, u32[]{:S(2)}) copy-start(f32[128]{0:T(128)S(1)} %add_rsqrt_fusion.1) | copy-start | bytes 1540
  170.7 1.4 copy-start.10
  173.0 81.1 %all-gather.11.cloned.1.call-start = ((), (), s32[]{:S(2)}) async-start(), calls=%async_computation.8 | async-start | bytes 3686400 | tf_op jit(solution)/shard_map/all_gather | solution.py:66
  175.8 140.1 %all-gather.13.cloned.1.call-start = ((), (), s32[]{:S(2)}) async-start(), calls=%async_computation.9 | async-start | bytes 6656000 | tf_op jit(solution)/shard_map/all_gather | solution.py:47
  176.4 330.3 %all-gather.15.cloned.1.call-start = ((), (), s32[]{:S(2)}) async-start(), calls=%async_computation.10 | async-start | bytes 25600000 | tf_op jit(solution)/shard_map/all_gather | solution.py:56
  177.0 527.2 %all-gather.17.cloned.1.call-start = ((), (), s32[]{:S(2)}) async-start(), calls=%async_computation.11 | async-start | bytes 26624000 | tf_op jit(solution)/shard_map/all_gather | solution.py:58
  177.6 929.8 %reduce-scatter.13.cloned.1.call-start = ((), (), s32[]{:S(2)}) async-start(), calls=%async_computation.12 | async-start | bytes 7372800 | tf_op jit(solution)/shard_map/reduce_scatter | solution.py:254
  178.1 328.6 %copy-start.24 = (f32[1600]{0:T(1024)}, f32[1600]{0:T(1024)S(1)}, u32[]{:S(2)}) copy-start(f32[1600]{0:T(1024)S(1)} %convert_element_type.124) | copy-start | bytes 19204
  273.2 4.7 copy-start
  287.4 4.7 copy-start
  295.8 24.9 copy-start.11
  320.7 408.2 %copy-start.3 = (f32[128,1600]{0,1:T(8,128)}, f32[128,1600]{0,1:T(8,128)S(1)}, u32[]{:S(2)}) copy-start(f32[128,1600]{0,1:T(8,128)S(1)} %get-tuple-element.367) | copy-start | bytes 2457604
  321.0 383.2 %copy-start.14 = (bf16[1,128,1600]{1,2,0:T(8,128)(2,1)S(1)}, bf16[1,128,1600]{1,2,0:T(8,128)(2,1)}, u32[]{:S(2)}) copy-start(bf16[1,128,1600]{1,2,0:T(8,128)(2,1)} %param.35) | copy-start | bytes 1228804
  716.2 12.7 copy-start.9
  730.2 4.4 copy-start.7
  1035.0 145.9 %reduce-scatter.15.cloned.1.call-start = ((), (), s32[]{:S(2)}) async-start(), calls=%async_computation.13 | async-start | bytes 7372800 | tf_op jit(solution)/shard_map/reduce_scatter | solution.py:257
  1042.3 247.1 %reduce-scatter.21.cloned.1.call-start = ((), (), s32[]{:S(2)}) async-start(), calls=%async_computation.16 | async-start | bytes 13312000
  1049.3 134.5 %copy-start.6 = (bf16[1,128,1600]{1,2,0:T(8,128)(2,1)S(1)}, bf16[1,128,1600]{1,2,0:T(8,128)(2,1)}, u32[]{:S(2)}) copy-start(bf16[1,128,1600]{1,2,0:T(8,128)(2,1)} %param.20) | copy-start | bytes 1228804
  1049.3 134.5 %copy-start.21 = (f32[1600]{0:T(1024)S(1)}, f32[1600]{0:T(1024)}, u32[]{:S(2)}) copy-start(f32[1600]{0:T(1024)} %copy-done.20) | copy-start | bytes 19204
  1049.3 134.5 %copy-start.23 = (f32[1600]{0:T(1024)S(1)}, f32[1600]{0:T(1024)}, u32[]{:S(2)}) copy-start(f32[1600]{0:T(1024)} %copy-done.22) | copy-start | bytes 19204
  1049.3 134.4 %copy-start.27 = (f32[128]{0:T(128)S(1)}, f32[128]{0:T(128)}, u32[]{:S(2)}) copy-start(f32[128]{0:T(128)} %copy-done.26) | copy-start | bytes 1540
  1049.3 134.4 %copy-start.29 = (f32[128]{0:T(128)S(1)}, f32[128]{0:T(128)}, u32[]{:S(2)}) copy-start(f32[128]{0:T(128)} %copy-done.28) | copy-start | bytes 1540
  1049.3 515.3 %reduce-scatter.19.cloned.1.call-start = ((), (), s32[]{:S(2)}) async-start(), calls=%async_computation.15 | async-start | bytes 38912000
  1050.4 146.6 %copy-start.16 = (bf16[128,25,64]{0,2,1:T(8,128)(2,1)}, bf16[128,25,64]{0,2,1:T(8,128)(2,1)S(1)}, u32[]{:S(2)}) copy-start(bf16[128,25,64]{0,2,1:T(8,128)(2,1)S(1)} %broadcast_multiply_fusion) | copy-start | bytes 1228804
  1108.5 88.5 %copy-start.18 = (bf16[128,1600]{0,1:T(8,128)(2,1)}, bf16[128,1600]{0,1:T(8,128)(2,1)S(1)}, u32[]{:S(2)}) copy-start(bf16[128,1600]{0,1:T(8,128)(2,1)S(1)} %convert_element_type.136) | copy-start | bytes 1228804
  1197.1 758.7 %reduce-scatter.23.cloned.1.call-start = ((), (), s32[]{:S(2)}) async-start(), calls=%async_computation.17 | async-start | bytes 51200000
  1217.1 1104.6 %reduce-scatter.17.cloned.1.call-start = ((), (), s32[]{:S(2)}) async-start(), calls=%async_computation.14 | async-start | bytes 53248000 | tf_op jit(solution)/shard_map/reduce_scatter | solution.py:71
  1237.7 1134.1 %all-reduce.30.cloned.1.call-start = ((), (), s32[]{:S(2)}) async-start(), calls=%async_computation.19 | async-start | bytes 188416
  1248.8 1734.6 %all-reduce.28.cloned.1.call-start = ((), (), s32[]{:S(2)}) async-start(), calls=%async_computation.18 | async-start | bytes 62668800 | tf_op jit(solution)/shard_map/psum | solution.py:288
  2983.4 7.1 copy-start.13
  2990.4 10.8 slice-start
  2991.9 9.3 slice-start.1
  2991.9 9.3 slice-start.2
  (12 other events, 11.8 us)
Sparse Core Ops, SparseCore 0:
  9.9 150.0 all-gather.6
  173.1 40.2 all-gather.8
  215.5 38.4 all-gather.10
  255.7 60.2 all-gather.12
  317.7 189.0 all-gather.14
  508.4 195.7 all-gather.16
  1035.1 72.1 reduce-scatter.12
  1110.2 70.6 reduce-scatter.14
  1184.6 104.6 reduce-scatter.20
  1292.4 272.1 reduce-scatter.18
  1567.7 388.0 reduce-scatter.22
  1958.7 362.9 reduce-scatter.16
  2326.8 44.9 all-reduce.29
  2374.6 608.7 all-reduce.27
where the time goes:
time: 3040 us; the launch traced here: 3010 us
  waiting for transfers between devices  2390 us (79%)
  local copies, waits for them, and re-layouts  332 us (11%)
  matrix products  199 us (7%)
  blocking collectives  49.8 us (2%)
    unnamed x18, waiting for transfers between devices  742 us
    psum x1, waiting for transfers between devices, shards(): lax.psum((small_grads[0], small_grads[1], grad_w_qkv, small_grads[2], sma...  574 us
    reduce_scatter x1, waiting for transfers between devices, owned_rows(): lax.psum_scatter(lax.dot_general(left, right, (((0,), (0,)), ((), ())), p...  366 us
    dynamic_update_slice x8, local copies, waits for them, and re-layouts, attend_back(): lax.scan(step, start_query, key_tiles)  249 us
    all_gather x1, waiting for transfers between devices, gather_mlp(): lax.all_gather(w_fc, 'fsdp', axis=0, tiled=True)  186 us
    all_gather x1, waiting for transfers between devices, gather_mlp(): lax.all_gather(w_out, 'fsdp', axis=0, tiled=True)  185 us
    all_gather x1, waiting for transfers between devices, gather_attention(): lax.all_gather(w_qkv, 'fsdp', axis=0, tiled=True)  128 us
    reduce_scatter x1, waiting for transfers between devices, shards(): lax.psum_scatter(value_terms.reshape(-1, model_width), 'ctx', scatter_dim...  72.4 us
  transfers between devices with their start and end apart: 14, of which 14 were waited for; matrix products, arithmetic and copies ran while one was open for 6% of the time, Pallas kernels for 0%

commit v1 on v0

v1 whole, which is shorter than its diff:
```python
from functools import partial

import jax
import jax.numpy as jnp
from jax import lax
from jax.experimental import pallas as pl
from jax.experimental.pallas import tpu as pltpu
from jax.sharding import PartitionSpec as P

HEADS = 25
HEAD = 64
EPSILON = 1e-05
MASKED = -1e30
BF = jnp.bfloat16
F32 = jnp.float32
BQ = 256


def matmul(left, right):
    return jnp.dot(left, right, preferred_element_type=F32)


def matmul_t(left, right):
    return lax.dot_general(left, right, (((1,), (1,)), ((), ())), preferred_element_type=F32)


def t_matmul(left, right):
    return lax.dot_general(left, right, (((0,), (0,)), ((), ())), preferred_element_type=F32)


def normalize(inputs):
    centred = inputs - jnp.mean(inputs, axis=-1, keepdims=True)
    inverse = lax.rsqrt(jnp.mean(centred * centred, axis=-1, keepdims=True) + EPSILON)
    return centred * inverse, inverse


def norm_back(grad_out, normed, inverse, gain):
    grad_norm = grad_out * gain
    mean_grad = jnp.mean(grad_norm, axis=-1, keepdims=True)
    mean_dot = jnp.mean(grad_norm * normed, axis=-1, keepdims=True)
    return inverse * (grad_norm - mean_grad - normed * mean_dot)


def gelu_pair(v):
    a = 0.7978845608028654
    inner = a * (v + 0.044715 * v * v * v)
    t = jnp.tanh(inner)
    value = 0.5 * v * (1.0 + t)
    slope = 0.5 * (1.0 + t) + 0.5 * v * (1.0 - t * t) * a * (1.0 + 3 * 0.044715 * v * v)
    return value, slope


def head_mask(width, head):
    lane = lax.broadcasted_iota(jnp.int32, (1, width), 1)
    return (lane >= head * HEAD) & (lane < (head + 1) * HEAD)


def sort_in(where_ref, blocks, blk, src, dst):
    for b in range(blocks):
        at = pl.multiple_of(where_ref[b] * blk, blk)
        dst[b * blk : (b + 1) * blk, :] = src[pl.ds(at, blk), :]


def each_block(length, step):
    if length <= 1024:
        for i in range(length // BQ):
            step(i * BQ, (i + 1) * BQ)
    else:
        pl.loop(0, length // BQ)(lambda i: step(pl.multiple_of(i * BQ, BQ), length))


def attend_kernel(blocks, blk, where_ref, q_ref, k_ref, v_ref, o_ref, lse_ref, q_s, k_s, v_s, o_s):
    length, width = q_ref.shape
    sort_in(where_ref, blocks, blk, q_ref, q_s)
    sort_in(where_ref, blocks, blk, k_ref, k_s)
    sort_in(where_ref, blocks, blk, v_ref, v_s)
    def step(base, ext):
        row = lax.broadcasted_iota(jnp.int32, (BQ, ext), 0) + base
        col = lax.broadcasted_iota(jnp.int32, (BQ, ext), 1)
        seen = col <= row
        now = pl.ds(base, BQ)
        q = q_s[now, :]
        total = None
        for h in range(width // HEAD):
            mine = head_mask(width, h)
            score = matmul_t(jnp.where(mine, q, 0).astype(BF), k_s[:ext, :])
            score = jnp.where(seen, score, MASKED)
            top = jnp.max(score, axis=1, keepdims=True)
            prob = jnp.exp(score - top)
            norm = jnp.sum(prob, axis=1, keepdims=True)
            out = matmul(prob.astype(BF), v_s[:ext, :]) / norm
            total = out if total is None else jnp.where(mine, out, total)
            lse = jnp.broadcast_to(top + jnp.log(norm), (BQ, 128))
            lse_ref[0, h : h + 1, now] = jnp.transpose(lse)[0:1, :]
        o_s[now, :] = total.astype(BF)

    each_block(length, step)
    for b in range(blocks):
        at = pl.multiple_of(where_ref[b] * blk, blk)
        o_ref[pl.ds(at, blk), :] = o_s[b * blk : (b + 1) * blk, :]


def attend_back_kernel(
    blocks, blk, where_ref, q_ref, k_ref, v_ref, g_ref, lse_ref, dq_ref, dk_ref, dv_ref,
    q_s, k_s, v_s, g_s, dq_s, dk_s, dv_s,
):
    length, width = q_ref.shape
    sort_in(where_ref, blocks, blk, q_ref, q_s)
    sort_in(where_ref, blocks, blk, k_ref, k_s)
    sort_in(where_ref, blocks, blk, v_ref, v_s)
    sort_in(where_ref, blocks, blk, g_ref, g_s)
    dk_s[...] = jnp.zeros_like(dk_s)
    dv_s[...] = jnp.zeros_like(dv_s)

    def step(base, ext):
        key = lax.broadcasted_iota(jnp.int32, (ext, BQ), 0)
        query = lax.broadcasted_iota(jnp.int32, (ext, BQ), 1) + base
        seen = key <= query
        now = pl.ds(base, BQ)
        q = q_s[now, :]
        g = g_s[now, :]
        dq_total = None
        for h in range(width // HEAD):
            mine = head_mask(width, h)
            q_h = jnp.where(mine, q, 0).astype(BF)
            g_h = jnp.where(mine, g, 0).astype(BF)
            score = matmul_t(k_s[:ext, :], q_h)
            prob = jnp.where(seen, jnp.exp(score - lse_ref[0, h : h + 1, now]), 0.0)
            grad_prob = matmul_t(v_s[:ext, :], g_h)
            delta = jnp.sum(prob * grad_prob, axis=0, keepdims=True)
            grad_score = (prob * (grad_prob - delta)).astype(BF)
            dv_s[:ext, :] += matmul(prob.astype(BF), g_h)
            dk_s[:ext, :] += matmul(grad_score, q_h)
            dq = t_matmul(grad_score, k_s[:ext, :])
            dq_total = dq if dq_total is None else jnp.where(mine, dq, dq_total)
        dq_s[now, :] = dq_total

    each_block(length, step)
    for b in range(blocks):
        at = pl.multiple_of(where_ref[b] * blk, blk)
        dq_ref[pl.ds(at, blk), :] = dq_s[b * blk : (b + 1) * blk, :].astype(BF)
        dk_ref[pl.ds(at, blk), :] = dk_s[b * blk : (b + 1) * blk, :].astype(BF)
        dv_ref[pl.ds(at, blk), :] = dv_s[b * blk : (b + 1) * blk, :].astype(BF)


def attention_specs(length, slots, blocks):
    width = 128 if slots % 2 == 0 else slots * HEAD
    groups = slots * HEAD // width
    part = lambda offset: pl.BlockSpec((length, width), lambda g, where: (0, offset * groups + g))
    lse = pl.BlockSpec((1, 8, length), lambda g, where: (g, 0, 0))
    return width, groups, part, lse


def attend(where, qkv, slots, blk):
    length = qkv.shape[0]
    blocks = length // blk
    width, groups, part, lse = attention_specs(length, slots, blocks)
    return pl.pallas_call(
        partial(attend_kernel, blocks, blk),
        out_shape=(
            jax.ShapeDtypeStruct((length, slots * HEAD), BF),
            jax.ShapeDtypeStruct((groups, 8, length), F32),
        ),
        grid_spec=pltpu.PrefetchScalarGridSpec(
            num_scalar_prefetch=1,
            grid=(groups,),
            in_specs=[part(0), part(1), part(2)],
            out_specs=[part(0), lse],
            scratch_shapes=[pltpu.VMEM((length, width), BF)] * 4,
        ),
        compiler_params=pltpu.CompilerParams(vmem_limit_bytes=60 << 20),
        cost_estimate=pl.CostEstimate(
            flops=4 * slots * length * length * HEAD,
            transcendentals=slots * length * length,
            bytes_accessed=8 * length * slots * HEAD,
        ),
        name="attend",
    )(where, qkv, qkv, qkv)


def attend_back(where, qkv, grad, lse_rows, slots, blk):
    length = qkv.shape[0]
    blocks = length // blk
    width, groups, part, lse = attention_specs(length, slots, blocks)
    return pl.pallas_call(
        partial(attend_back_kernel, blocks, blk),
        out_shape=(jax.ShapeDtypeStruct((length, slots * HEAD), BF),) * 3,
        grid_spec=pltpu.PrefetchScalarGridSpec(
            num_scalar_prefetch=1,
            grid=(groups,),
            in_specs=[part(0), part(1), part(2), part(0), lse],
            out_specs=[part(0)] * 3,
            scratch_shapes=[pltpu.VMEM((length, width), BF)] * 4
            + [pltpu.VMEM((length, width), F32)] * 3,
        ),
        compiler_params=pltpu.CompilerParams(vmem_limit_bytes=60 << 20),
        cost_estimate=pl.CostEstimate(
            flops=10 * slots * length * length * HEAD,
            transcendentals=slots * length * length,
            bytes_accessed=14 * length * slots * HEAD,
        ),
        name="attend_back",
    )(where, qkv, qkv, qkv, grad, lse_rows)


def shards(
    m,
    n,
    layer_input,
    pair_blocks,
    ln1_gain,
    ln1_bias,
    w_qkv,
    bias_q,
    bias_v,
    w_proj,
    bias_proj,
    ln2_gain,
    ln2_bias,
    w_fc,
    bias_fc,
    w_out,
    bias_out,
    cotangent,
):
    rows = layer_input.shape[1]
    width = layer_input.shape[2]
    length = rows * n
    blk = rows // 2
    units = w_out.shape[0]
    own_rows = w_qkv.shape[0]
    scale = HEAD ** (-0.5)
    f = lax.axis_index("fsdp")
    c = lax.axis_index("ctx")

    def swap_f(v, mask):
        return lax.ppermute(v, "fsdp", [(i, i ^ mask) for i in range(m)]) if mask else v

    def gather_f(v):
        return [swap_f(v, mask) for mask in range(m)]

    def settle_f(pieces):
        size = pieces[0].shape[0]
        whole = jnp.zeros((m * size,) + pieces[0].shape[1:], pieces[0].dtype)
        for mask, piece in enumerate(pieces):
            whole = lax.dynamic_update_slice_in_dim(whole, piece, (f ^ mask) * size, 0)
        return whole

    def sum_f(total):
        result = total[:rows]
        for mask in range(1, m):
            sent = total[mask * rows : (mask + 1) * rows].astype(BF)
            result = result + swap_f(sent, mask).astype(F32)
        return result

    slots = 2 * -(-HEADS // (2 * n))
    span = slots * HEAD
    bounds = [HEADS * i // n for i in range(n + 1)]
    starts = [min(bounds[i], HEADS - slots) for i in range(n)]
    kept = [
        slice((bounds[i] - starts[i]) * HEAD, (bounds[i + 1] - starts[i]) * HEAD) for i in range(n)
    ]
    holders = [i for i in range(n) if bounds[i + 1] > bounds[i]]
    first = jnp.minimum(HEADS * c // n, HEADS - slots)
    head = first + lax.broadcasted_iota(jnp.int32, (1, span), 1) // HEAD
    owned = ((head >= HEADS * c // n) & (head < HEADS * (c + 1) // n)).astype(F32)

    blocks = 2 * n
    flat = pair_blocks.reshape(-1)
    index = jnp.arange(blocks, dtype=jnp.int32)
    where = jnp.sum(jnp.where(flat[None, :] == index[:, None], index[None, :], 0), axis=1)

    x = layer_input[0]
    cot = cotangent[0]
    small = jnp.stack(
        [ln1_gain, ln1_bias, bias_q, bias_v, bias_proj, ln2_gain, ln2_bias, bias_out]
    )
    small = settle_f([v[None] for v in gather_f(small)])
    small = jnp.transpose(small, (1, 0, 2)).reshape(8, width).astype(F32)
    gain_one, shift_one, all_bias_q, all_bias_v, all_bias_proj, gain_two, shift_two, all_bias_out = (
        small[i] for i in range(8)
    )
    slice_qkv = lax.dynamic_slice_in_dim(
        w_qkv.reshape(own_rows, 3, width), first * HEAD, span, 2
    ).reshape(own_rows, 3 * span)
    head_qkv = lax.all_gather(slice_qkv, "fsdp", axis=0, tiled=True)
    head_bias_q = lax.dynamic_slice_in_dim(all_bias_q, first * HEAD, span, 0)
    head_bias_v = lax.dynamic_slice_in_dim(all_bias_v, first * HEAD, span, 0)
    full_proj = lax.all_gather(w_proj, "fsdp", axis=0, tiled=True)
    unit_fc = settle_f(
        [
            swap_f(lax.dynamic_slice_in_dim(w_fc, (f ^ mask) * units, units, 1), mask)
            for mask in range(m)
        ]
    )
    cots = jnp.concatenate(gather_f(cot), axis=0)

    all_x = lax.all_gather(x, "ctx", axis=0, tiled=True).astype(F32)
    h1 = (normalize(all_x)[0] * gain_one + shift_one).astype(BF)
    projected = matmul(h1, head_qkv)
    qkv = jnp.concatenate(
        [
            (projected[:, :span] + head_bias_q) * scale,
            projected[:, span : 2 * span],
            projected[:, 2 * span :] + head_bias_v,
        ],
        axis=1,
    ).astype(BF)
    head_context, lse = attend(where, qkv, slots, blk)
    sent = lax.all_to_all(head_context.reshape(n, rows, span), "ctx", 0, 0)
    context = jnp.concatenate(
        [sent[i][:, kept[i]] for i in holders], axis=1
    )
    xs = x.astype(F32)
    mixed = xs + (matmul(context, full_proj) + all_bias_proj)

    normed_two, inverse_two = normalize(mixed)
    h2 = (normed_two * gain_two + shift_two).astype(BF)
    h2s = jnp.concatenate(gather_f(h2), axis=0)
    hidden = matmul(h2s, unit_fc) + bias_fc.astype(F32)
    value, slope = gelu_pair(hidden)
    activated = value.astype(BF)
    result = (mixed + sum_f(matmul(activated, w_out)) + all_bias_out).astype(BF)

    grad_hidden = (matmul_t(cots, w_out) * slope).astype(BF)
    grad_h2 = sum_f(matmul_t(grad_hidden, unit_fc))
    grad_w_out = t_matmul(activated, cots).astype(BF)
    grad_w_fc = t_matmul(h2s, grad_hidden).astype(BF)
    grad_bias_fc = jnp.sum(grad_hidden.astype(F32), axis=0)
    grad_mixed = cot.astype(F32) + norm_back(grad_h2, normed_two, inverse_two, gain_two)

    part_out = lax.psum_scatter(grad_w_out, "ctx", scatter_dimension=0, tiled=True)
    out_grad_w_out = lax.all_gather(part_out, "ctx", axis=0, tiled=True).astype(F32)
    part_fc = lax.psum_scatter(grad_w_fc, "ctx", scatter_dimension=0, tiled=True)
    share = n // m
    route = [
        (i * n + j, (j // share) * n + i * share + j % share) for i in range(m) for j in range(n)
    ]
    part_fc = lax.ppermute(part_fc, ("fsdp", "ctx"), route)
    all_fc = lax.all_gather(part_fc, "ctx", axis=0, tiled=False)
    all_fc = all_fc.reshape(m, share, width // n, units).transpose(1, 2, 0, 3)
    out_grad_w_fc = all_fc.reshape(own_rows, m * units).astype(F32)

    grad_attended = grad_mixed.astype(BF)
    grad_context = matmul_t(grad_attended, full_proj).astype(BF)
    sent_back = jnp.stack(
        [grad_context[:, starts[i] * HEAD : starts[i] * HEAD + span] for i in range(n)]
    )
    grad_heads = lax.all_to_all(sent_back, "ctx", 0, 0).reshape(length, span)
    grad_heads = (grad_heads * owned.astype(BF)).astype(BF)
    grad_query, grad_keys, grad_values = attend_back(where, qkv, grad_heads, lse, slots, blk)
    grad_qkv = jnp.concatenate([grad_query * BF(scale), grad_keys, grad_values], axis=1)

    rows_proj = jnp.concatenate(
        [
            swap_f(lax.dynamic_slice_in_dim(context, (f ^ mask) * own_rows, own_rows, 1), mask)
            for mask in range(m)
        ],
        axis=0,
    )
    grad_w_proj = t_matmul(rows_proj, jnp.concatenate(gather_f(grad_attended), axis=0)).astype(BF)
    out_grad_w_proj = lax.psum(grad_w_proj, "ctx").astype(F32)

    partial_h1 = matmul_t(grad_qkv, head_qkv)
    grad_h1 = lax.psum_scatter(partial_h1.astype(BF), "ctx", scatter_dimension=0, tiled=True)
    grad_h1 = grad_h1.astype(F32)
    normed_one, inverse_one = normalize(xs)
    grad_stream = grad_mixed + norm_back(grad_h1, normed_one, inverse_one, gain_one)

    grad_head_qkv = t_matmul(h1, grad_qkv)
    mine = lax.psum_scatter(grad_head_qkv.astype(BF), "fsdp", scatter_dimension=0, tiled=True)
    gathered = lax.all_gather(mine, "ctx", axis=0, tiled=False).reshape(n, own_rows, 3, span)
    out_grad_w_qkv = jnp.concatenate(
        [
            gathered[i, :, kind, kept[i]]
            for kind in range(3)
            for i in holders
        ],
        axis=1,
    ).astype(F32)

    def spread(v):
        whole = jnp.zeros((width,), F32)
        return lax.dynamic_update_slice_in_dim(whole, v * owned[0], first * HEAD, 0)

    sums = jnp.stack(
        [
            jnp.sum(grad_h1 * normed_one, axis=0),
            jnp.sum(grad_h1, axis=0),
            spread(jnp.sum(grad_query.astype(F32), axis=0) * scale),
            spread(jnp.sum(grad_values.astype(F32), axis=0)),
            jnp.sum(grad_attended.astype(F32), axis=0),
            jnp.sum(grad_h2 * normed_two, axis=0),
            jnp.sum(grad_h2, axis=0),
            jnp.sum(cot.astype(F32), axis=0),
        ]
    )
    sums = lax.psum(sums, ("fsdp", "ctx"))
    sums = lax.dynamic_slice_in_dim(sums, f * own_rows, own_rows, 1)
    out_bias_fc = lax.psum(grad_bias_fc, "ctx")
    return (
        result[None],
        grad_stream.astype(BF)[None],
        sums[0],
        sums[1],
        out_grad_w_qkv,
        sums[2],
        sums[3],
        out_grad_w_proj,
        sums[4],
        sums[5],
        sums[6],
        out_grad_w_fc,
        out_bias_fc,
        out_grad_w_out,
        sums[7],
    )


def solution(mesh):
    tokens = P("fsdp", "ctx", None)
    vector = P("fsdp")
    matrix = P("fsdp", None)
    in_specs = (
        (tokens, P(), vector, vector, matrix, vector, vector, matrix, vector)
        + (vector, vector, matrix, vector, matrix, vector, tokens)
    )
    out_specs = (
        (tokens, tokens, vector, vector, matrix, vector, vector, matrix, vector)
        + (vector, vector, matrix, vector, matrix, vector)
    )
    body = partial(shards, mesh.shape["fsdp"], mesh.shape["ctx"])
    return jax.shard_map(
        body, mesh=mesh, in_specs=in_specs, out_specs=out_specs, check_vma=False
    )
```

time: 3040 us -> 882 us (0.29)
  waiting for transfers between devices: 2390 us -> 418 us
  local copies, waits for them, and re-layouts: 332 us -> 160 us
  matrix products: 199 us -> 66 us
  blocking collectives: 49.8 us -> 106 us
  starting transfers between devices: 0.74 us -> 47 us
    unnamed x18 -> x14, waiting for transfers between devices: 742 us -> 156 us
    psum x1, waiting for transfers between devices: 574 us -> 17.6 us  [shards(): out_grad_w_proj = lax.psum(grad_w_proj, 'ctx').astype(F32)]
    reduce_scatter x3 -> x1, waiting for transfers between devices: 495 us -> 0.02 us  [shards(): lax.psum_scatter(grad_head_qkv.astype(BF), 'fsdp', scatter_dimension=0, t...]
    all_gather x6, waiting for transfers between devices: 582 us -> 156 us  [the longest x1 85 us: shards(): full_proj = lax.all_gather(w_proj, 'fsdp', axis=0, tiled=True)]
    dynamic_update_slice x8 -> x9, local copies, waits for them, and re-layouts: 249 us -> 7.96 us  [the longest x7 7.63 us: settle_f(): whole = lax.dynamic_update_slice_in_dim(whole, piece, (f ^ mask) * size, 0)]
    dot_general x22 -> x8, matrix products: 160 us -> 45.2 us  [the longest x4 26 us: t_matmul(): lax.dot_general(left, right, (((0,), (0,)), ((), ())), preferred_element_...]
    psum x1 -> x2, blocking collectives: 30.5 us -> 106 us  [the longest x1 62.9 us: shards(): out_bias_fc = lax.psum(grad_bias_fc, 'ctx')]
    ppermute x0 -> x25, waiting for transfers between devices: none -> 65.7 us  [the longest x24 65.7 us: swap_f(): lax.ppermute(v, 'fsdp', [(i, i ^ mask) for i in range(m)])]
  transfers between devices with their start and end apart: 14 -> 38, of which waited for: 14 -> 20; matrix products, arithmetic and copies ran while one was open for 6% -> 23% of each run, Pallas kernels for 0% -> 1%
where the time goes in v1:
time: 882 us; the launch traced here: 871 us
  waiting for transfers between devices  418 us (47%)
  local copies, waits for them, and re-layouts  160 us (18%)
  blocking collectives  106 us (12%)
  matrix products  66 us (7%)
  starting transfers between devices  47 us (5%)
  other arithmetic  35.3 us (4%)
  Pallas kernels  23.1 us (3%)
  between operations  15.4 us (2%)
    unnamed x14, waiting for transfers between devices  156 us
    all_gather x1, waiting for transfers between devices, shards(): full_proj = lax.all_gather(w_proj, 'fsdp', axis=0, tiled=True)  85 us
    ppermute x24, waiting for transfers between devices, swap_f(): lax.ppermute(v, 'fsdp', [(i, i ^ mask) for i in range(m)])  65.7 us
    psum x1, blocking collectives, shards(): out_bias_fc = lax.psum(grad_bias_fc, 'ctx')  62.9 us
    psum x1, blocking collectives, shards(): sums = lax.psum(sums, ('fsdp', 'ctx'))  42.8 us
    all_gather x1, waiting for transfers between devices, shards(): head_qkv = lax.all_gather(slice_qkv, 'fsdp', axis=0, tiled=True)  40.7 us
    ppermute x24, starting transfers between devices, swap_f(): lax.ppermute(v, 'fsdp', [(i, i ^ mask) for i in range(m)])  30.4 us
    slice x6, local copies, waits for them, and re-layouts, shards(): gathered[i, :, kind, kept[i]]  28.7 us
  transfers between devices with their start and end apart: 38, of which 20 were waited for; matrix products, arithmetic and copies ran while one was open for 23% of the time, Pallas kernels for 1%

profile of v1, /device:TPU:0, one launch (start us, length us, event | category | flops | bytes accessed | tf_op | source)
XLA Modules:
  0.0 870.6 jit_solution(1867513711003518801)
XLA Ops:
  8.0 11.4 %reshape.228 = bf16[400,3,1600]{2,1,0:T(4,128)(2,1)} reshape(bf16[400,4800]{1,0:T(8,128)(2,1)} %param.20) | data formatting | bytes 7680000 | tf_op jit(solution)/shard_map/reshape | solution.py:284
  30.7 7.9 constant_dynamic-slice_fusion.5
  42.0 10.5 %all-gather.16.cloned.1.call-done = bf16[1,1024,1600]{1,2,0:T(8,128)(2,1)} async-done(((bf16[1,128,1600]{1,2,0:T(8,128)(2,1)}), bf16[1,1024,1600]{1,2,0:T(8,128)(2,1)}) %all-gather.16.cloned.1.call-update) | async-done | bytes 3276816 | tf_op jit(solution)/shard_map/all_gather | solution.py:298
  56.4 40.7 %all-gather.10.cloned.1.call-done = bf16[1600,768]{1,0:T(8,128)(2,1)} async-done(((bf16[400,768]{1,0:T(8,128)(2,1)}), bf16[1600,768]{1,0:T(8,128)(2,1)}) %all-gather.10.cloned.1.call-update) | async-done | bytes 2457616 | tf_op jit(solution)/shard_map/all_gather | solution.py:286
  97.1 5.3 fusion.75
  104.0 9.9 %attend.1 = (bf16[1024,256]{1,0:T(8,128)(2,1)}, f32[2,8,1024]{2,1,0:T(8,128)}) custom-call(s32[16]{0:T(128)} %select_reduce_fusion.where_ref, bf16[1024,768]{1,0:T(8,128)(2,1)} %pad_maximum_fusion.2.q_ref.k_ref.v_ref, bf16[1024,768]{1,0:T(8,128)(2,1)} %pad_maximum_fusion.2.q_ref.k_ref.v_ref, bf16[1024,768]{1,0:T(8,128)(2,1)} %pad_maximum_fusion.2.q_ref.k_ref.v_ref), custom_call_target="tpu_custom_call" | custom-call | flops 1073741824 | bytes 2097152 | tf_op jit(solution)/shard_map/attend/pallas_call | solution.py:158
  113.9 4.7 all-to-all-start
  125.8 8.1 all-to-all-done
  134.2 85.0 %all-gather.12.cloned.1.call-done = bf16[1600,1600]{1,0:T(8,128)(2,1)} async-done(((bf16[400,1600]{1,0:T(8,128)(2,1)}), bf16[1600,1600]{1,0:T(8,128)(2,1)}) %all-gather.12.cloned.1.call-update) | async-done | bytes 5120016 | tf_op jit(solution)/shard_map/all_gather | solution.py:289
  219.2 4.8 fusion.85
  233.8 4.3 collective-permute-done.5
  239.5 6.4 collective-permute-done.4
  246.7 5.8 convolution_add_fusion
  252.6 3.3 fusion.87
  255.9 7.3 convert_reduce_fusion.1
  263.2 5.7 fusion.86
  276.0 6.5 collective-permute-done.17
  284.0 7.4 collective-permute-done.16
  292.3 7.8 collective-permute-done.11
  300.1 7.6 collective-permute-done.10
  316.5 4.6 all-to-all-start.1
  321.6 14.8 %all-to-all-done.1 = bf16[8,128,256]{1,2,0:T(8,128)(2,1)S(1)} async-done(((bf16[8,128,256]{1,2,0:T(8,128)(2,1)}), bf16[8,128,256]{1,2,0:T(8,128)(2,1)S(1)}, u32[]{:S(2)}, u32[]{:S(2)}) %all-to-all-start.1) | async-done | bytes 524320 | tf_op jit(solution)/shard_map/all_to_all | solution.py:349
  338.1 13.2 %attend_back.1 = (bf16[1024,256]{1,0:T(8,128)(2,1)}, bf16[1024,256]{1,0:T(8,128)(2,1)}, bf16[1024,256]{1,0:T(8,128)(2,1)}) custom-call(s32[16]{0:T(128)} %select_reduce_fusion.where_ref, bf16[1024,768]{1,0:T(8,128)(2,1)} %pad_maximum_fusion.2.q_ref.k_ref.v_ref, bf16[1024,768]{1,0:T(8,128)(2,1)} %pad_maximum_fusion.2.q_ref.k_ref.v_ref, ...), custom_call_target="tpu_custom_call" | custom-call | flops 2684354560 | bytes 3670016 | tf_op jit(solution)/shard_map/attend_back/pallas_call | solution.py:185
  353.2 6.9 convolution_convert_fusion.3
  360.2 8.3 convolution_convert_fusion
  369.5 7.5 convolution_convert_fusion.1
  384.0 21.2 %collective-permute-done.20 = bf16[128,400]{1,0:T(8,128)(2,1)S(1)} collective-permute-done((bf16[128,400]{1,0:T(8,128)(2,1)S(1)}, bf16[128,400]{1,0:T(8,128)(2,1)S(1)}, u32[]{:S(2)}, u32[]{:S(2)}) %collective-permute-start.20) | collective-permute-done | bytes 102432 | tf_op jit(solution)/shard_map/ppermute | solution.py:237
  410.1 3.3 convolution_convert_fusion.4
  413.6 6.3 convolution_convert_fusion.2
  419.9 5.5 copy.282
  426.2 48.7 %reduce-scatter.17.cloned.1.call-done = bf16[200,1600]{1,0:T(8,128)(2,1)} async-done(((bf16[1600,1600]{1,0:T(8,128)(2,1)}), bf16[200,1600]{1,0:T(8,128)(2,1)}) %reduce-scatter.17.cloned.1.call-update) | async-done | bytes 640016
  475.0 62.8 %reduce-scatter.15.cloned.1.call-done = bf16[200,1600]{1,0:T(8,128)(2,1)} async-done(((bf16[1600,1600]{1,0:T(8,128)(2,1)}), bf16[200,1600]{1,0:T(8,128)(2,1)}) %reduce-scatter.15.cloned.1.call-update) | async-done | bytes 640016
  537.7 6.7 collective-permute-start.24
  545.9 62.9 %psum.23 = f32[1600]{0:T(1024)} all-reduce(f32[1600]{0:T(1024)S(1)} %copy-done.27), channel_id=1, replica_groups=mesh['fsdp'=4,'ctx'=8] {'ctx'}, use_global_device_ids=true, to_apply=%region_25.26 | all-reduce | flops 1600 | bytes 12800 | tf_op jit(solution)/shard_map/psum | solution.py:400
  609.7 17.6 %all-reduce.4.cloned.1.call-done = bf16[400,1600]{1,0:T(8,128)(2,1)} async-done(((bf16[400,1600]{1,0:T(8,128)(2,1)}), bf16[400,1600]{1,0:T(8,128)(2,1)}) %all-reduce.4.cloned.1.call-update) | async-done | bytes 1280016 | tf_op jit(solution)/shard_map/psum | solution.py:362
  630.2 42.7 %reduce-scatter.13.cloned.1.call-done = bf16[128,1600]{1,0:T(8,128)(2,1)} async-done(((bf16[1024,1600]{1,0:T(8,128)(2,1)}), bf16[128,1600]{1,0:T(8,128)(2,1)}) %reduce-scatter.13.cloned.1.call-update) | async-done | bytes 409616
  676.4 42.8 %psum.21 = f32[8,1600]{1,0:T(8,128)S(1)} all-reduce(f32[8,1600]{1,0:T(8,128)S(1)} %stack.104), channel_id=1, replica_groups=mesh['fsdp'=4,'ctx'=8] {'fsdp','ctx'}, use_global_device_ids=true, to_apply=%region_20.21 | all-reduce | flops 12800 | bytes 102400 | tf_op jit(solution)/shard_map/psum | solution.py:398
  719.9 7.5 all-gather.18.cloned.1.call-done
  727.4 7.5 copy.234
  734.9 17.0 %reshape.232 = bf16[8,400,3,256]{1,0,3,2:T(8,128)(2,1)} reshape(bf16[3200,768]{0,1:T(8,128)(2,1)} %copy.234) | data formatting | bytes 9830400 | tf_op jit(solution)/shard_map/reshape | solution.py:372
  756.6 19.3 %fusion.80 = (bf16[1,400,1,192]{1,0,3,2:T(2,128)(2,1)S(1)}, bf16[1,400,1,192]{1,0,3,2:T(2,128)(2,1)S(1)}, bf16[1,400,1,192]{1,0,3,2:T(2,128)(2,1)S(1)}, bf16[1,4...) fusion(bf16[8,400,3,256]{1,0,3,2:T(8,128)(2,1)} %reshape.232), kind=kLoop, calls=%fused_computation.188 | loop fusion | bytes 5836800 | tf_op jit(solution)/shard_map/slice | solution.py:375
  781.9 4.5 fusion.79
  808.4 7.8 concatenate.30
  816.2 5.9 convert_element_type.168
  822.0 7.4 convert_element_type.178
  829.5 11.9 %all-gather.20.cloned.1.call-done = bf16[1600,1600]{1,0:T(8,128)(2,1)} async-done(((bf16[200,1600]{1,0:T(8,128)(2,1)}), bf16[1600,1600]{1,0:T(8,128)(2,1)}) %all-gather.20.cloned.1.call-update) | async-done | bytes 5120016 | tf_op jit(solution)/shard_map/all_gather | solution.py:340
  844.6 6.7 copy.259
  851.3 12.4 %reshape.233 = f32[400,6400]{1,0:T(8,128)} reshape(f32[2,200,4,1600]{3,2,1,0:T(4,128)} %copy.259) | data formatting | bytes 20480000 | tf_op jit(solution)/shard_map/convert_element_type | solution.py:342
  (312 shorter events, 121.4 us)
Async XLA Ops:
  7.2 45.4 %all-gather.16.cloned.1.call-start = ((), (), s32[]{:S(2)}) async-start(), calls=%async_computation.11 | async-start | bytes 3686400 | tf_op jit(solution)/shard_map/all_gather | solution.py:298
  7.9 89.2 %all-gather.10.cloned.1.call-start = ((), (), s32[]{:S(2)}) async-start(), calls=%async_computation.6 | async-start | bytes 3072000 | tf_op jit(solution)/shard_map/all_gather | solution.py:286
  22.4 196.8 %all-gather.12.cloned.1.call-start = ((), (), s32[]{:S(2)}) async-start(), calls=%async_computation.7 | async-start | bytes 6656000 | tf_op jit(solution)/shard_map/all_gather | solution.py:289
  23.4 17.9 %collective-permute-start = (bf16[8,400]{1,0:T(8,128)(2,1)S(1)}, bf16[8,400]{1,0:T(8,128)(2,1)S(1)}, u32[]{:S(2)}, u32[]{:S(2)}) collective-permute-start(bf16[8,400]{1,0:T(8,128)(2,1)S(1)} %stack.87), channel_id=1, source_target_pairs={{0,8},{8,0},{16,24},{24,16},{1,9},{9,1},{17,25},{25,17},{2,10},{10... | collective-permute-start | bytes 19208 | tf_op jit(solution)/shard_map/ppermute | solution.py:237
  26.4 14.9 %collective-permute-start.1 = (bf16[8,400]{1,0:T(8,128)(2,1)S(1)}, bf16[8,400]{1,0:T(8,128)(2,1)S(1)}, u32[]{:S(2)}, u32[]{:S(2)}) collective-permute-start(bf16[8,400]{1,0:T(8,128)(2,1)S(1)} %stack.87), channel_id=1, source_target_pairs={{0,16},{8,24},{16,0},{24,8},{1,17},{9,25},{17,1},{25,9},{2,18},{10... | collective-permute-start | bytes 19208 | tf_op jit(solution)/shard_map/ppermute | solution.py:237
  27.9 13.4 %collective-permute-start.2 = (bf16[8,400]{1,0:T(8,128)(2,1)S(1)}, bf16[8,400]{1,0:T(8,128)(2,1)S(1)}, u32[]{:S(2)}, u32[]{:S(2)}) collective-permute-start(bf16[8,400]{1,0:T(8,128)(2,1)S(1)} %stack.87), channel_id=1, source_target_pairs={{0,24},{8,16},{16,8},{24,0},{1,25},{9,17},{17,9},{25,1},{2,26},{10... | collective-permute-start | bytes 19208 | tf_op jit(solution)/shard_map/ppermute | solution.py:237
  38.5 84.8 %collective-permute-start.6 = (bf16[400,1600]{1,0:T(8,128)(2,1)}, bf16[400,1600]{1,0:T(8,128)(2,1)}, u32[]{:S(2)}, u32[]{:S(2)}) collective-permute-start(bf16[400,1600]{1,0:T(8,128)(2,1)} %get-tuple-element.114), channel_id=1, source_target_pairs={{0,8},{8,0},{16,24},{24,16},{1,9},{9,1},{17,25},{25,17},{2,10},{10... | collective-permute-start | bytes 3840008 | tf_op jit(solution)/shard_map/ppermute | solution.py:237
  113.9 105.3 %copy-start = (bf16[1,128,1600]{1,2,0:T(8,128)(2,1)S(1)}, bf16[1,128,1600]{1,2,0:T(8,128)(2,1)}, u32[]{:S(2)}) copy-start(bf16[1,128,1600]{1,2,0:T(8,128)(2,1)} %param.16) | copy-start | bytes 1228804
  113.9 20.1 %all-to-all-start = ((bf16[8,128,256]{2,1,0:T(8,128)(2,1)}), bf16[8,128,256]{2,1,0:T(8,128)(2,1)S(1)}, u32[]{:S(2)}, u32[]{:S(2)}) async-start(bf16[8,128,256]{2,1,0:T(8,128)(2,1)} %bitcast.222), calls=%async_computation | async-start | bytes 1048576 | tf_op jit(solution)/shard_map/all_to_all | solution.py:310
  118.6 109.1 %collective-permute-start.7 = (bf16[400,1600]{1,0:T(8,128)(2,1)}, bf16[400,1600]{1,0:T(8,128)(2,1)}, u32[]{:S(2)}, u32[]{:S(2)}) collective-permute-start(bf16[400,1600]{1,0:T(8,128)(2,1)} %get-tuple-element.116), channel_id=1, source_target_pairs={{0,16},{8,24},{16,0},{24,8},{1,17},{9,25},{17,1},{25,9},{2,18},{10... | collective-permute-start | bytes 3840008 | tf_op jit(solution)/shard_map/ppermute | solution.py:237
  120.1 110.7 %collective-permute-start.8 = (bf16[400,1600]{1,0:T(8,128)(2,1)}, bf16[400,1600]{1,0:T(8,128)(2,1)}, u32[]{:S(2)}, u32[]{:S(2)}) collective-permute-start(bf16[400,1600]{1,0:T(8,128)(2,1)} %get-tuple-element.113), channel_id=1, source_target_pairs={{0,24},{8,16},{16,8},{24,0},{1,25},{9,17},{17,9},{25,1},{2,26},{10... | collective-permute-start | bytes 3840008 | tf_op jit(solution)/shard_map/ppermute | solution.py:237
  121.5 134.3 %collective-permute-start.14 = (bf16[128,1600]{0,1:T(8,128)(2,1)S(1)}, bf16[128,1600]{0,1:T(8,128)(2,1)}, u32[]{:S(2)}, u32[]{:S(2)}) collective-permute-start(bf16[128,1600]{0,1:T(8,128)(2,1)S(1)} %bitcast.193), channel_id=1, source_target_pairs={{0,24},{8,16},{16,8},{24,0},{1,25},{9,17},{17,9},{25,1},{2,26},{10... | collective-permute-start | bytes 1228808 | tf_op jit(solution)/shard_map/ppermute | solution.py:237
  224.0 83.7 %copy-start.23 = (f32[128]{0:T(128)}, f32[128]{0:T(128)S(1)}, u32[]{:S(2)}) copy-start(f32[128]{0:T(128)S(1)} %broadcast_multiply_fusion.8) | copy-start | bytes 1540
  224.2 83.5 %copy-start.25 = (f32[128]{0:T(128)}, f32[128]{0:T(128)S(1)}, u32[]{:S(2)}) copy-start(f32[128]{0:T(128)S(1)} %add_rsqrt_fusion.2) | copy-start | bytes 1540
  224.7 13.3 %collective-permute-start.5 = (bf16[128,1600]{0,1:T(8,128)(2,1)S(1)}, bf16[128,1600]{0,1:T(8,128)(2,1)S(1)}, u32[]{:S(2)}, u32[]{:S(2)}) collective-permute-start(bf16[128,1600]{0,1:T(8,128)(2,1)S(1)} %add_convert_fusion), channel_id=1, source_target_pairs={{0,24},{8,16},{16,8},{24,0},{1,25},{9,17},{17,9},{25,1},{2,26},{10... | collective-permute-start | bytes 1228808 | tf_op jit(solution)/shard_map/ppermute | solution.py:237
  226.3 19.6 %collective-permute-start.4 = (bf16[128,1600]{0,1:T(8,128)(2,1)S(1)}, bf16[128,1600]{0,1:T(8,128)(2,1)S(1)}, u32[]{:S(2)}, u32[]{:S(2)}) collective-permute-start(bf16[128,1600]{0,1:T(8,128)(2,1)S(1)} %add_convert_fusion), channel_id=1, source_target_pairs={{0,16},{8,24},{16,0},{24,8},{1,17},{9,25},{17,1},{25,9},{2,18},{10... | collective-permute-start | bytes 1228808 | tf_op jit(solution)/shard_map/ppermute | solution.py:237
  227.8 18.1 %collective-permute-start.3 = (bf16[128,1600]{0,1:T(8,128)(2,1)S(1)}, bf16[128,1600]{0,1:T(8,128)(2,1)S(1)}, u32[]{:S(2)}, u32[]{:S(2)}) collective-permute-start(bf16[128,1600]{0,1:T(8,128)(2,1)S(1)} %add_convert_fusion), channel_id=1, source_target_pairs={{0,8},{8,0},{16,24},{24,16},{1,9},{9,1},{17,25},{25,17},{2,10},{10... | collective-permute-start | bytes 1228808 | tf_op jit(solution)/shard_map/ppermute | solution.py:237
  230.8 25.1 %collective-permute-start.13 = (bf16[128,1600]{0,1:T(8,128)(2,1)S(1)}, bf16[128,1600]{0,1:T(8,128)(2,1)S(1)}, u32[]{:S(2)}, u32[]{:S(2)}) collective-permute-start(bf16[128,1600]{0,1:T(8,128)(2,1)S(1)} %bitcast.194), channel_id=1, source_target_pairs={{0,16},{8,24},{16,0},{24,8},{1,17},{9,25},{17,1},{25,9},{2,18},{10... | collective-permute-start | bytes 1228808 | tf_op jit(solution)/shard_map/ppermute | solution.py:237
  238.1 17.8 %collective-permute-start.12 = (bf16[128,1600]{0,1:T(8,128)(2,1)S(1)}, bf16[128,1600]{0,1:T(8,128)(2,1)S(1)}, u32[]{:S(2)}, u32[]{:S(2)}) collective-permute-start(bf16[128,1600]{0,1:T(8,128)(2,1)S(1)} %bitcast.195), channel_id=1, source_target_pairs={{0,8},{8,0},{16,24},{24,16},{1,9},{9,1},{17,25},{25,17},{2,10},{10... | collective-permute-start | bytes 1228808 | tf_op jit(solution)/shard_map/ppermute | solution.py:237
  269.1 13.3 %collective-permute-start.17 = (bf16[128,1600]{0,1:T(8,128)(2,1)S(1)}, bf16[128,1600]{0,1:T(8,128)(2,1)S(1)}, u32[]{:S(2)}, u32[]{:S(2)}) collective-permute-start(bf16[128,1600]{0,1:T(8,128)(2,1)S(1)} %get-tuple-element.120), channel_id=1, source_target_pairs={{0,24},{8,16},{16,8},{24,0},{1,25},{9,17},{17,9},{25,1},{2,26},{10... | collective-permute-start | bytes 1228808 | tf_op jit(solution)/shard_map/ppermute | solution.py:237
  271.6 19.8 %collective-permute-start.16 = (bf16[128,1600]{0,1:T(8,128)(2,1)S(1)}, bf16[128,1600]{0,1:T(8,128)(2,1)S(1)}, u32[]{:S(2)}, u32[]{:S(2)}) collective-permute-start(bf16[128,1600]{0,1:T(8,128)(2,1)S(1)} %get-tuple-element.121), channel_id=1, source_target_pairs={{0,16},{8,24},{16,0},{24,8},{1,17},{9,25},{17,1},{25,9},{2,18},{10... | collective-permute-start | bytes 1228808 | tf_op jit(solution)/shard_map/ppermute | solution.py:237
  272.2 19.1 %collective-permute-start.15 = (bf16[128,1600]{0,1:T(8,128)(2,1)S(1)}, bf16[128,1600]{0,1:T(8,128)(2,1)S(1)}, u32[]{:S(2)}, u32[]{:S(2)}) collective-permute-start(bf16[128,1600]{0,1:T(8,128)(2,1)S(1)} %get-tuple-element.119), channel_id=1, source_target_pairs={{0,8},{8,0},{16,24},{24,16},{1,9},{9,1},{17,25},{25,17},{2,10},{10... | collective-permute-start | bytes 1228808 | tf_op jit(solution)/shard_map/ppermute | solution.py:237
  272.9 27.2 %collective-permute-start.11 = (bf16[128,1600]{0,1:T(8,128)(2,1)S(1)}, bf16[128,1600]{0,1:T(8,128)(2,1)S(1)}, u32[]{:S(2)}, u32[]{:S(2)}) collective-permute-start(bf16[128,1600]{0,1:T(8,128)(2,1)S(1)} %get-tuple-element.123), channel_id=1, source_target_pairs={{0,24},{8,16},{16,8},{24,0},{1,25},{9,17},{17,9},{25,1},{2,26},{10... | collective-permute-start | bytes 1228808 | tf_op jit(solution)/shard_map/ppermute | solution.py:237
  275.3 32.4 %collective-permute-start.10 = (bf16[128,1600]{0,1:T(8,128)(2,1)S(1)}, bf16[128,1600]{0,1:T(8,128)(2,1)S(1)}, u32[]{:S(2)}, u32[]{:S(2)}) collective-permute-start(bf16[128,1600]{0,1:T(8,128)(2,1)S(1)} %get-tuple-element.124), channel_id=1, source_target_pairs={{0,16},{8,24},{16,0},{24,8},{1,17},{9,25},{17,1},{25,9},{2,18},{10... | collective-permute-start | bytes 1228808 | tf_op jit(solution)/shard_map/ppermute | solution.py:237
  282.5 25.2 %collective-permute-start.9 = (bf16[128,1600]{0,1:T(8,128)(2,1)S(1)}, bf16[128,1600]{0,1:T(8,128)(2,1)S(1)}, u32[]{:S(2)}, u32[]{:S(2)}) collective-permute-start(bf16[128,1600]{0,1:T(8,128)(2,1)S(1)} %get-tuple-element.122), channel_id=1, source_target_pairs={{0,8},{8,0},{16,24},{24,16},{1,9},{9,1},{17,25},{25,17},{2,10},{10... | collective-permute-start | bytes 1228808 | tf_op jit(solution)/shard_map/ppermute | solution.py:237
  316.5 19.9 %all-to-all-start.1 = ((bf16[8,128,256]{1,2,0:T(8,128)(2,1)}), bf16[8,128,256]{1,2,0:T(8,128)(2,1)S(1)}, u32[]{:S(2)}, u32[]{:S(2)}) async-start(bf16[8,128,256]{1,2,0:T(8,128)(2,1)} %fusion.54), calls=%async_computation.1 | async-start | bytes 1048576 | tf_op jit(solution)/shard_map/all_to_all | solution.py:349
  321.1 104.4 %reduce-scatter.11.cloned.1.call-start = ((), (), s32[]{:S(2)}) async-start(), calls=%async_computation.8 | async-start | bytes 3072000 | tf_op jit(solution)/shard_map/reduce_scatter | solution.py:371
  360.2 114.7 %reduce-scatter.17.cloned.1.call-start = ((), (), s32[]{:S(2)}) async-start(), calls=%async_computation.16 | async-start | bytes 5990400
  368.6 169.1 %reduce-scatter.15.cloned.1.call-start = ((), (), s32[]{:S(2)}) async-start(), calls=%async_computation.15 | async-start | bytes 5990400
  377.1 250.2 %all-reduce.4.cloned.1.call-start = ((), (), s32[]{:S(2)}) async-start(), calls=%async_computation.9 | async-start | bytes 2662400 | tf_op jit(solution)/shard_map/psum | solution.py:362
  378.0 32.1 %collective-permute-start.23 = (bf16[128,1600]{0,1:T(8,128)(2,1)S(1)}, bf16[128,1600]{0,1:T(8,128)(2,1)S(1)}, u32[]{:S(2)}, u32[]{:S(2)}) collective-permute-start(bf16[128,1600]{0,1:T(8,128)(2,1)S(1)} %copy-done.17), channel_id=1, source_target_pairs={{0,24},{8,16},{16,8},{24,0},{1,25},{9,17},{17,9},{25,1},{2,26},{10... | collective-permute-start | bytes 1228808 | tf_op jit(solution)/shard_map/ppermute | solution.py:237
  379.5 30.6 %collective-permute-start.22 = (bf16[128,1600]{0,1:T(8,128)(2,1)S(1)}, bf16[128,1600]{0,1:T(8,128)(2,1)S(1)}, u32[]{:S(2)}, u32[]{:S(2)}) collective-permute-start(bf16[128,1600]{0,1:T(8,128)(2,1)S(1)} %copy-done.17), channel_id=1, source_target_pairs={{0,16},{8,24},{16,0},{24,8},{1,17},{9,25},{17,1},{25,9},{2,18},{10... | collective-permute-start | bytes 1228808 | tf_op jit(solution)/shard_map/ppermute | solution.py:237
  380.1 30.0 %collective-permute-start.21 = (bf16[128,1600]{0,1:T(8,128)(2,1)S(1)}, bf16[128,1600]{0,1:T(8,128)(2,1)S(1)}, u32[]{:S(2)}, u32[]{:S(2)}) collective-permute-start(bf16[128,1600]{0,1:T(8,128)(2,1)S(1)} %copy-done.17), channel_id=1, source_target_pairs={{0,8},{8,0},{16,24},{24,16},{1,9},{9,1},{17,25},{25,17},{2,10},{10... | collective-permute-start | bytes 1228808 | tf_op jit(solution)/shard_map/ppermute | solution.py:237
  381.8 23.3 %collective-permute-start.20 = (bf16[128,400]{1,0:T(8,128)(2,1)S(1)}, bf16[128,400]{1,0:T(8,128)(2,1)S(1)}, u32[]{:S(2)}, u32[]{:S(2)}) collective-permute-start(bf16[128,400]{1,0:T(8,128)(2,1)S(1)} %get-tuple-element.135), channel_id=1, source_target_pairs={{0,24},{8,16},{16,8},{24,0},{1,25},{9,17},{17,9},{25,1},{2,26},{10... | collective-permute-start | bytes 307208 | tf_op jit(solution)/shard_map/ppermute | solution.py:237
  383.3 24.5 %collective-permute-start.19 = (bf16[128,400]{1,0:T(8,128)(2,1)S(1)}, bf16[128,400]{1,0:T(8,128)(2,1)S(1)}, u32[]{:S(2)}, u32[]{:S(2)}) collective-permute-start(bf16[128,400]{1,0:T(8,128)(2,1)S(1)} %get-tuple-element.136), channel_id=1, source_target_pairs={{0,16},{8,24},{16,0},{24,8},{1,17},{9,25},{17,1},{25,9},{2,18},{10... | collective-permute-start | bytes 307208 | tf_op jit(solution)/shard_map/ppermute | solution.py:237
  405.1 5.0 collective-permute-start.18
  413.5 259.4 %reduce-scatter.13.cloned.1.call-start = ((), (), s32[]{:S(2)}) async-start(), calls=%async_computation.14 | async-start | bytes 3833856
  425.3 120.6 %copy-start.27 = (f32[1600]{0:T(1024)S(1)}, f32[1600]{0:T(1024)}, u32[]{:S(2)}) copy-start(f32[1600]{0:T(1024)} %get-tuple-element.154) | copy-start | bytes 19204
  425.3 183.5 %copy-start.20 = (f32[1600]{0:T(1024)S(1)}, f32[1600]{0:T(1024)}, u32[]{:S(2)}) copy-start(f32[1600]{0:T(1024)} %get-tuple-element.86) | copy-start | bytes 19204
  425.3 183.7 %copy-start.2 = (bf16[1024,256]{1,0:T(8,128)(2,1)S(1)}, bf16[1024,256]{1,0:T(8,128)(2,1)}, u32[]{:S(2)}) copy-start(bf16[1024,256]{1,0:T(8,128)(2,1)} %get-tuple-element.22) | copy-start | bytes 1572868
  425.4 302.1 %all-gather.18.cloned.1.call-start = ((), (), s32[]{:S(2)}) async-start(), calls=%async_computation.12 | async-start | bytes 5529600 | tf_op jit(solution)/shard_map/all_gather | solution.py:372
  426.1 395.9 %all-gather.14.cloned.1.call-start = ((), (), s32[]{:S(2)}) async-start(), calls=%async_computation.10 | async-start | bytes 5990400 | tf_op jit(solution)/shard_map/all_gather | solution.py:333
  474.9 366.5 %all-gather.20.cloned.1.call-start = ((), (), s32[]{:S(2)}) async-start(), calls=%async_computation.13 | async-start | bytes 5990400 | tf_op jit(solution)/shard_map/all_gather | solution.py:340
  537.7 6.7 collective-permute-start.24
  609.0 65.8 %copy-start.24 = (f32[128]{0:T(128)S(1)}, f32[128]{0:T(128)}, u32[]{:S(2)}) copy-start(f32[128]{0:T(128)} %copy-done.23) | copy-start | bytes 1540
  609.1 65.8 %copy-start.26 = (f32[128]{0:T(128)S(1)}, f32[128]{0:T(128)}, u32[]{:S(2)}) copy-start(f32[128]{0:T(128)} %copy-done.25) | copy-start | bytes 1540
  609.1 65.8 %copy-start.32 = (f32[128]{0:T(128)S(1)}, f32[128]{0:T(128)}, u32[]{:S(2)}) copy-start(f32[128]{0:T(128)} %copy-done.30) | copy-start | bytes 1540
  609.1 65.8 %copy-start.37 = (f32[128]{0:T(128)S(1)}, f32[128]{0:T(128)}, u32[]{:S(2)}) copy-start(f32[128]{0:T(128)} %copy-done.36) | copy-start | bytes 1540
  (52 other events, 752.2 us)
Sparse Core Ops, SparseCore 0:
  9.6 42.9 all-gather.15
  55.0 42.0 all-gather.9
  98.9 120.2 all-gather.11
  360.3 51.7 reduce-scatter.10
  414.8 60.0 reduce-scatter.16
  477.6 60.0 reduce-scatter.14
  540.1 87.0 all-reduce.3
  630.1 42.7 reduce-scatter.12
  674.6 52.8 all-gather.17
  728.9 55.3 all-gather.13
  785.9 55.4 all-gather.19
